TPU v7x, 32 devices: a whole 2x2x4 slice. The times are simulated.
32 devices in a mesh: gx: 2 (over x), gy: 4 (over y, core), gz: 4 (over z).
Axes of the slice: x: 2, y: 2, z: 4, core: 2. Of those that a mesh axis runs over, the one named last changes fastest.
Arguments:
- charges: bfloat16 [8, 16, 16, 32, 128], P('gx', 'gy', 'gz'), may hold values from -6 to 6
- counts: int32 [8, 16, 16], P('gx', 'gy', 'gz'), may hold values from 32 to 128, as said below
- near_offsets: int32 [27, 3], replicated, may hold values from -1 to 1, as said below
- near_blocks: bfloat16 [27, 128, 128], replicated, may hold values from -0.109375 to 0.109375
- leaf_basis: bfloat16 [48, 128], replicated, may hold values from -0.5 to 0.5
- transfer: bfloat16 [8, 48, 48], replicated, may hold values from -0.625 to 0.625
- far_offsets: int32 [2, 32, 3], replicated, may hold values from -2 to 2, as said below
- coupling: bfloat16 [2, 32, 48, 48], replicated, may hold values from -0.15625 to 0.15625
- coarse_coupling: bfloat16 [2, 4, 4, 48, 48], replicated, may hold values from -0.3125 to 0.3125
Outputs:
- potentials: float32 [8, 16, 16, 32, 128], P('gx', 'gy', 'gz')
Inputs may be any that keep to these rules, and one draw needn't show every extreme that they name: `counts`: in each device's block of 4 x 4 x 4 leaf boxes some box holds 128 points. `near_offsets`: each of the 27 offsets with components in -1, 0, 1 appears once. `far_offsets`: each level lists 32 distinct offsets whose largest component in magnitude is 2.
All inputs are finite; a program needn't handle non-finite values.
Results may differ from a plain program's by a relative error of at most 0.008.
Values may be sent and summed in bfloat16 or wider, within the bound.
A program may use at most 128 MiB of HBM per device.

v0:
```python
import jax
import jax.numpy as jnp
from jax import lax
from jax.sharding import PartitionSpec as P


def extended_2(value, sides, width):
    for axis, dim in sides:
        size, length = (lax.axis_size(axis), value.shape[dim])
        up = [(i, (i + 1) % size) for i in range(size)]
        down = [(j, i) for i, j in up]
        last = lax.slice_in_dim(value, length - width, length, axis=dim)
        leading = lax.slice_in_dim(value, 0, width, axis=dim)
        before = lax.ppermute(last, axis, up)
        after = lax.ppermute(leading, axis, down)
        value = jnp.concatenate([before, value, after], axis=dim)
    return value


def take_window(extended, margin, offset, extent):
    start = offset + margin
    corner = [start[0], start[1], start[2]] + [jnp.int32(0)] * (extended.ndim - 3)
    return lax.dynamic_slice(extended, corner, tuple(extent) + tuple(extended.shape[3:]))


def near_field(extended, margin, near_offsets, near_blocks, extent):
    stacked = jax.vmap(lambda offset: take_window(extended, margin, offset, extent))(near_offsets)
    return jnp.einsum("sxyzrq,spq->xyzrp", stacked, near_blocks, preferred_element_type=jnp.float32)


def far_couple(extended, margin, offsets, matrices, extent, rank_count):
    stacked = jax.vmap(lambda offset: take_window(extended, margin, offset, extent))(offsets)
    stacked = stacked.reshape(stacked.shape[:4] + (rank_count, -1))
    return jnp.einsum("kij,kxyzjr->xyzir", matrices, stacked, preferred_element_type=jnp.float32)


def leaf_moments(masked, leaf_basis):
    return jnp.einsum(
        "kp,xyzrp->xyzkr", leaf_basis, masked, preferred_element_type=jnp.float32
    ).astype(jnp.bfloat16)


def flatten(moments):
    return moments.reshape(moments.shape[:3] + (-1,))


def upward(moments, transfer):
    first_len, second_len, third_len, rank_count, columns = moments.shape
    split = moments.reshape(
        first_len // 2, 2, second_len // 2, 2, third_len // 2, 2, rank_count, columns
    )
    kids = split.transpose(0, 2, 4, 1, 3, 5, 6, 7).reshape(
        first_len // 2, second_len // 2, third_len // 2, 8, rank_count, columns
    )
    return jnp.einsum(
        "ckj,xyzcjr->xyzkr", transfer, kids, preferred_element_type=jnp.float32
    ).astype(jnp.bfloat16)


def downward(parent, transfer):
    rounded = parent.astype(jnp.bfloat16)
    kids = jnp.einsum("cjk,xyzjr->xyzckr", transfer, rounded, preferred_element_type=jnp.float32)
    first_len, second_len, third_len, rank_count, columns = parent.shape
    split = kids.reshape(first_len, second_len, third_len, 2, 2, 2, rank_count, columns)
    return split.transpose(0, 3, 1, 4, 2, 5, 6, 7).reshape(
        2 * first_len, 2 * second_len, 2 * third_len, rank_count, columns
    )


def coarse_couple(moments_two, coarse_coupling, place, sizes):
    depth, rank_count, columns = moments_two.shape[2:]
    rows = moments_two.reshape(depth, rank_count * columns)
    index_x, index_y, index_z = place
    count_x, count_y, count_z = sizes
    grid_x, grid_y, grid_z = coarse_coupling.shape[:3]
    flat_coupling = coarse_coupling.reshape(grid_x * grid_y * grid_z, rank_count, rank_count)
    own_z = index_z * depth + jnp.arange(depth, dtype=jnp.int32)
    piece = lax.all_gather(rows, ("gx", "gy", "gz"), axis=0, tiled=True)
    number = jnp.arange(piece.shape[0], dtype=jnp.int32)
    device = number // depth
    source_x = device // (count_y * count_z)
    source_y = device // count_z % count_y
    source_z = device % count_z * depth + number % depth
    off_x = (source_x - index_x) % grid_x
    off_y = (source_y - index_y) % grid_y
    off_z = (source_z[:, None] - own_z[None, :]) % grid_z
    flat_index = (off_x[:, None] * grid_y + off_y[:, None]) * grid_z + off_z
    mats = jnp.take(flat_coupling, flat_index, axis=0)
    values = piece.reshape(piece.shape[0], rank_count, columns)
    local_two = jnp.einsum("acij,ajr->cir", mats, values, preferred_element_type=jnp.float32)
    return local_two.reshape(moments_two.shape)


def body(
    charges,
    counts,
    near_offsets,
    near_blocks,
    leaf_basis,
    transfer,
    far_offsets,
    coupling,
    coarse_coupling,
):
    extent = charges.shape[:3]
    rank_count = leaf_basis.shape[0]
    capacity = charges.shape[4]
    place = (lax.axis_index("gx"), lax.axis_index("gy"), lax.axis_index("gz"))
    sizes = (lax.axis_size("gx"), lax.axis_size("gy"), lax.axis_size("gz"))
    live = (jnp.arange(capacity, dtype=jnp.int32) < counts[..., None]).astype(jnp.bfloat16)
    masked = charges * live[:, :, :, None, :]
    beside = extended_2(masked, (("gx", 0), ("gy", 1), ("gz", 2)), 1)
    own_moments = leaf_moments(masked, leaf_basis)
    moments_wide = extended_2(flatten(own_moments), (("gx", 0), ("gy", 1), ("gz", 2)), 2)
    near = near_field(beside, 1, near_offsets, near_blocks, extent)
    local_zero = far_couple(moments_wide, 2, far_offsets[0], coupling[0], extent, rank_count)
    moments_one = upward(own_moments, transfer)
    wide_one = extended_2(flatten(moments_one), (("gx", 0), ("gy", 1), ("gz", 2)), 2)
    local_one = far_couple(
        wide_one, 2, far_offsets[1], coupling[1], moments_one.shape[:3], rank_count
    )
    moments_two = upward(moments_one, transfer)
    local_two = coarse_couple(moments_two, coarse_coupling, place, sizes)
    total_one = local_one + downward(local_two, transfer)
    total_zero = local_zero + downward(total_one, transfer)
    far = jnp.einsum(
        "kp,xyzkr->xyzrp",
        leaf_basis,
        total_zero.astype(jnp.bfloat16),
        preferred_element_type=jnp.float32,
    )
    return (near + far) * live[:, :, :, None, :].astype(jnp.float32)


def solution(mesh):
    in_specs = (
        P("gx", "gy", "gz", None, None),
        P("gx", "gy", "gz"),
        P(),
        P(),
        P(),
        P(),
        P(),
        P(),
        P(),
    )
    out_specs = P("gx", "gy", "gz", None, None)
    return jax.shard_map(body, mesh=mesh, in_specs=in_specs, out_specs=out_specs, check_vma=False)
```

profile of v0, /device:TPU:0, one launch (start us, length us, event | category | flops | bytes accessed | tf_op | source)
XLA Modules:
  0.0 389.2 jit_solution(513155457398799025)
XLA Ops:
  3.7 3.0 collective-permute-start.12
  14.4 67.5 %all-gather = bf16[32,1,1536]{2,1,0:T(2,128)(2,1)S(1)} all-gather(bf16[1,1,1536]{2,1,0:T(2,128)(2,1)S(1)} %reshape.419), channel_id=1, replica_groups=mesh['gx'=2,'gy'=4,'gz'=4] {'gx','gy','gz'}, dimensions={0}, use_global_device_ids=true | all-gather | bytes 101376 | tf_op jit(solution)/shard_map/all_gather | solution.py:78
  93.6 3.8 collective-permute-start.17
  106.7 99.8 %while.3 = (s32[]{:T(128)}, bf16[6,6,6,1536]{3,2,1,0:T(8,128)(2,1)S(1)}, s32[32,4]{0,1:T(4,128)S(1)}, bf16[32,2,2,2,1536]{4,3,2,1,0:T(2,128)(2,1)}, s32[]{:T(128)}) while((s32[]{:T(128)}, bf16[6,6,6,1536]{3,2,1,0:T(8,128)(2,1)S(1)}, s32[32,4]{0,1:T(4,128)S(1)}, bf16[32,2,2,2,1536]{4,3,2,1,0:T(2,128)(2,1)}, s32[]{:T(128)}) %tuple.49), condition=%wide.while_cond.1, body=%wide.while_body.1.sunk | while | flops 2 | bytes 51321 | solution.py:23
  206.6 5.2 %reshape.437 = bf16[32,2,2,2,48,32]{5,4,3,2,1,0:T(8,128)(2,1)} reshape(bf16[32,2,2,2,1536]{4,3,2,1,0:T(2,128)(2,1)} %get-tuple-element.20) | data formatting | bytes 1572864 | tf_op jit(solution)/shard_map/reshape | solution.py:33
  212.7 3.8 collective-permute-start.5
  216.6 3.1 fusion.14
  220.7 4.0 %collective-permute-done.4 = bf16[6,6,1,32,128]{4,3,2,1,0:T(8,128)(2,1)} collective-permute-done((bf16[6,6,1,32,128]{4,3,2,1,0:T(8,128)(2,1)}, bf16[6,6,1,32,128]{4,3,2,1,0:T(8,128)(2,1)}, u32[]{:S(2)}, u32[]{:S(2)}) %collective-permute-start.4) | collective-permute-done | bytes 294944 | tf_op jit(solution)/shard_map/ppermute | solution.py:14
  228.0 7.0 %gather_fusion = bf16[27,4,4,4,32,128]{5,4,3,2,1,0:T(8,128)(2,1)} fusion(bf16[6,6,6,32,128]{4,3,2,1,0:T(8,128)(2,1)S(1)} %pad_maximum_fusion, s32[27]{0:T(128)S(1)} %fusion.68), kind=kCustom, calls=%fused_computation | custom fusion | bytes 28312092 | tf_op jit(solution)/shard_map/vmap()/gather | solution.py:23
  235.0 7.5 %fusion = f32[4,4,4,32,128,1]{4,3,1,0,2,5:T(8,128)S(1)} fusion(bf16[27,4,4,4,32,128]{5,4,3,2,1,0:T(8,128)(2,1)} %gather_fusion, bf16[27,128,128]{2,1,0:T(8,128)(2,1)S(1)} %copy-done), kind=kOutput, calls=%fused_computation.6 | convolution fusion | flops 1811939328 | bytes 16089088 | tf_op jit(solution)/shard_map/sxyzrq,spq->xyzrp/dot_general | solution.py:28
  244.9 102.1 %while.2 = (s32[]{:T(128)}, bf16[8,8,8,1536]{3,2,1,0:T(8,128)(2,1)S(1)}, s32[32,4]{0,1:T(4,128)S(1)}, bf16[32,4,4,4,1536]{4,3,2,1,0:T(4,128)(2,1)}, s32[]{:T(128)}) while((s32[]{:T(128)}, bf16[8,8,8,1536]{3,2,1,0:T(8,128)(2,1)S(1)}, s32[32,4]{0,1:T(4,128)S(1)}, bf16[32,4,4,4,1536]{4,3,2,1,0:T(4,128)(2,1)}, s32[]{:T(128)}) %tuple.52), condition=%wide.while_cond, body=%wide.while_body.sunk | while | flops 2 | bytes 395385 | solution.py:23
  245.6 2.6 bitcast_dynamic-update-slice_fusion.4
  248.8 2.6 bitcast_dynamic-update-slice_fusion.4
  267.9 2.6 bitcast_dynamic-update-slice_fusion.4
  271.1 2.6 bitcast_dynamic-update-slice_fusion.4
  296.6 2.6 bitcast_dynamic-update-slice_fusion.4
  309.3 2.6 bitcast_dynamic-update-slice_fusion.4
  312.5 2.6 bitcast_dynamic-update-slice_fusion.4
  328.5 2.6 bitcast_dynamic-update-slice_fusion.4
  331.7 2.6 bitcast_dynamic-update-slice_fusion.4
  338.1 2.6 bitcast_dynamic-update-slice_fusion.4
  344.4 2.6 bitcast_dynamic-update-slice_fusion.4
  347.0 29.0 %reshape.436 = bf16[32,4,4,4,48,32]{5,4,3,2,1,0:T(8,128)(2,1)} reshape(bf16[32,4,4,4,1536]{4,3,2,1,0:T(4,128)(2,1)} %get-tuple-element.12) | data formatting | bytes 12582912 | tf_op jit(solution)/shard_map/reshape | solution.py:33
  376.0 11.9 %fusion.3 = bf16[4,4,4,48,32]{3,4,2,1,0:T(8,128)(2,1)S(1)} fusion(f32[4,4,4,48,32]{3,4,2,1,0:T(8,128)S(1)} %bitcast.189, bf16[32,4,4,4,48,32]{5,4,3,2,1,0:T(8,128)(2,1)} %reshape.436, bf16[2,32,48,48]{3,2,1,0:T(8,128)(2,1)} %param.16), kind=kOutput, calls=%fused_computation.12 | convolution fusion | flops 302186496 | bytes 26148864 | tf_op jit(solution)/shard_map/kij,kxyzjr->xyzir/dot_general | solution.py:34
  (298 shorter events, 214.6 us)
Async XLA Ops:
  0.0 235.0 %copy-start = (bf16[27,128,128]{2,1,0:T(8,128)(2,1)S(1)}, bf16[27,128,128]{2,1,0:T(8,128)(2,1)}, u32[]{:S(2)}) copy-start(bf16[27,128,128]{2,1,0:T(8,128)(2,1)} %param.12) | copy-start | bytes 2654212
  3.1 79.5 %copy-start.14 = (s32[27,3]{0,1:T(4,128)S(1)}, s32[27,3]{0,1:T(4,128)}, u32[]{:S(2)}) copy-start(s32[27,3]{0,1:T(4,128)} %param.11) | copy-start | bytes 976
  3.7 82.1 %collective-permute-start.12 = (bf16[2,2,2,1536]{3,2,1,0:T(2,128)(2,1)S(1)}, bf16[2,2,2,1536]{3,2,1,0:T(2,128)(2,1)S(1)}, u32[]{:S(2)}, u32[]{:S(2)}) collective-permute-start(bf16[2,2,2,1536]{3,2,1,0:T(2,128)(2,1)S(1)} %reshape.343), channel_id=1, source_target_pairs={{0,16},{16,0},{1,17},{17,1},{2,18},{18,2},{3,19},{19,3},{4,20},{20... | collective-permute-start | bytes 73736 | tf_op jit(solution)/shard_map/ppermute | solution.py:14
  6.7 80.7 %collective-permute-start.13 = (bf16[2,2,2,1536]{3,2,1,0:T(2,128)(2,1)S(1)}, bf16[2,2,2,1536]{3,2,1,0:T(2,128)(2,1)S(1)}, u32[]{:S(2)}, u32[]{:S(2)}) collective-permute-start(bf16[2,2,2,1536]{3,2,1,0:T(2,128)(2,1)S(1)} %reshape.343), channel_id=1, source_target_pairs={{16,0},{0,16},{17,1},{1,17},{18,2},{2,18},{19,3},{3,19},{20,4},{4,... | collective-permute-start | bytes 73736 | tf_op jit(solution)/shard_map/ppermute | solution.py:15
  8.0 79.5 %collective-permute-start.6 = (bf16[2,4,4,1536]{3,2,1,0:T(4,128)(2,1)}, bf16[2,4,4,1536]{3,2,1,0:T(4,128)(2,1)}, u32[]{:S(2)}, u32[]{:S(2)}) collective-permute-start(bf16[2,4,4,1536]{3,2,1,0:T(4,128)(2,1)} %slice.91), channel_id=1, source_target_pairs={{0,16},{16,0},{1,17},{17,1},{2,18},{18,2},{3,19},{19,3},{4,20},{20... | collective-permute-start | bytes 294920 | tf_op jit(solution)/shard_map/ppermute | solution.py:14
  11.1 79.2 %collective-permute-start.7 = (bf16[2,4,4,1536]{3,2,1,0:T(4,128)(2,1)}, bf16[2,4,4,1536]{3,2,1,0:T(4,128)(2,1)}, u32[]{:S(2)}, u32[]{:S(2)}) collective-permute-start(bf16[2,4,4,1536]{3,2,1,0:T(4,128)(2,1)} %slice.93), channel_id=1, source_target_pairs={{16,0},{0,16},{17,1},{1,17},{18,2},{2,18},{19,3},{3,19},{20,4},{4,... | collective-permute-start | bytes 294920 | tf_op jit(solution)/shard_map/ppermute | solution.py:15
  11.9 81.7 %collective-permute-start = (bf16[1,4,4,32,128]{4,3,2,1,0:T(8,128)(2,1)}, bf16[1,4,4,32,128]{4,3,2,1,0:T(8,128)(2,1)S(1)}, u32[]{:S(2)}, u32[]{:S(2)}) collective-permute-start(bf16[1,4,4,32,128]{4,3,2,1,0:T(8,128)(2,1)} %get-tuple-element.51), channel_id=1, source_target_pairs={{0,16},{16,0},{1,17},{17,1},{2,18},{18,2},{3,19},{19,3},{4,20},{20... | collective-permute-start | bytes 393224 | tf_op jit(solution)/shard_map/ppermute | solution.py:14
  85.8 11.6 %collective-permute-start.1 = (bf16[1,4,4,32,128]{4,3,2,1,0:T(8,128)(2,1)}, bf16[1,4,4,32,128]{4,3,2,1,0:T(8,128)(2,1)S(1)}, u32[]{:S(2)}, u32[]{:S(2)}) collective-permute-start(bf16[1,4,4,32,128]{4,3,2,1,0:T(8,128)(2,1)} %get-tuple-element.52), channel_id=1, source_target_pairs={{16,0},{0,16},{17,1},{1,17},{18,2},{2,18},{19,3},{3,19},{20,4},{4,... | collective-permute-start | bytes 393224 | tf_op jit(solution)/shard_map/ppermute | solution.py:15
  87.5 4.0 %collective-permute-start.14 = (bf16[6,2,2,1536]{3,2,1,0:T(2,128)(2,1)S(1)}, bf16[6,2,2,1536]{3,2,1,0:T(2,128)(2,1)S(1)}, u32[]{:S(2)}, u32[]{:S(2)}) collective-permute-start(bf16[6,2,2,1536]{3,2,1,0:T(2,128)(2,1)S(1)} %constant_dynamic-update-slice_fusion.3), channel_id=1, source_target_pairs={{0,4},{4,8},{8,12},{12,0},{1,5},{5,9},{9,13},{13,1},{2,6},{6,10},{... | collective-permute-start | bytes 221192 | tf_op jit(solution)/shard_map/ppermute | solution.py:14
  87.6 5.7 %collective-permute-start.15 = (bf16[6,2,2,1536]{3,2,1,0:T(2,128)(2,1)S(1)}, bf16[6,2,2,1536]{3,2,1,0:T(2,128)(2,1)S(1)}, u32[]{:S(2)}, u32[]{:S(2)}) collective-permute-start(bf16[6,2,2,1536]{3,2,1,0:T(2,128)(2,1)S(1)} %constant_dynamic-update-slice_fusion.3), channel_id=1, source_target_pairs={{4,0},{8,4},{12,8},{0,12},{5,1},{9,5},{13,9},{1,13},{6,2},{10,6},{... | collective-permute-start | bytes 221192 | tf_op jit(solution)/shard_map/ppermute | solution.py:15
  91.3 15.5 %copy-start.3 = (bf16[8,4,4,1536]{3,2,1,0:T(4,128)(2,1)}, bf16[8,4,4,1536]{3,2,1,0:T(4,128)(2,1)S(1)}, u32[]{:S(2)}) copy-start(bf16[8,4,4,1536]{3,2,1,0:T(4,128)(2,1)S(1)} %constant_dynamic-update-slice_fusion) | copy-start | bytes 1179652
  91.4 6.8 %collective-permute-start.8 = (bf16[8,2,4,1536]{3,2,1,0:T(4,128)(2,1)S(1)}, bf16[8,2,4,1536]{3,2,1,0:T(4,128)(2,1)S(1)}, u32[]{:S(2)}, u32[]{:S(2)}) collective-permute-start(bf16[8,2,4,1536]{3,2,1,0:T(4,128)(2,1)S(1)} %get-tuple-element.53), channel_id=1, source_target_pairs={{0,4},{4,8},{8,12},{12,0},{1,5},{5,9},{9,13},{13,1},{2,6},{6,10},{... | collective-permute-start | bytes 589832 | tf_op jit(solution)/shard_map/ppermute | solution.py:14
  91.5 8.5 %collective-permute-start.9 = (bf16[8,2,4,1536]{3,2,1,0:T(4,128)(2,1)S(1)}, bf16[8,2,4,1536]{3,2,1,0:T(4,128)(2,1)S(1)}, u32[]{:S(2)}, u32[]{:S(2)}) collective-permute-start(bf16[8,2,4,1536]{3,2,1,0:T(4,128)(2,1)S(1)} %get-tuple-element.54), channel_id=1, source_target_pairs={{4,0},{8,4},{12,8},{0,12},{5,1},{9,5},{13,9},{1,13},{6,2},{10,6},{... | collective-permute-start | bytes 589832 | tf_op jit(solution)/shard_map/ppermute | solution.py:15
  93.5 10.2 %collective-permute-start.16 = (bf16[6,6,2,1536]{3,2,1,0:T(2,128)(2,1)S(1)}, bf16[6,6,2,1536]{3,2,1,0:T(2,128)(2,1)S(1)}, u32[]{:S(2)}, u32[]{:S(2)}) collective-permute-start(bf16[6,6,2,1536]{3,2,1,0:T(2,128)(2,1)S(1)} %pad_maximum_fusion.9), channel_id=1, source_target_pairs={{0,1},{1,2},{2,3},{3,0},{4,5},{5,6},{6,7},{7,4},{8,9},{9,10},{10,1... | collective-permute-start | bytes 663560 | tf_op jit(solution)/shard_map/ppermute | solution.py:14
  93.6 12.4 %collective-permute-start.17 = (bf16[6,6,2,1536]{3,2,1,0:T(2,128)(2,1)S(1)}, bf16[6,6,2,1536]{3,2,1,0:T(2,128)(2,1)S(1)}, u32[]{:S(2)}, u32[]{:S(2)}) collective-permute-start(bf16[6,6,2,1536]{3,2,1,0:T(2,128)(2,1)S(1)} %pad_maximum_fusion.9), channel_id=1, source_target_pairs={{1,0},{2,1},{3,2},{0,3},{5,4},{6,5},{7,6},{4,7},{9,8},{10,9},{11,1... | collective-permute-start | bytes 663560 | tf_op jit(solution)/shard_map/ppermute | solution.py:15
  98.2 113.5 %collective-permute-start.2 = (bf16[6,1,4,32,128]{4,3,2,1,0:T(8,128)(2,1)}, bf16[6,1,4,32,128]{4,3,2,1,0:T(8,128)(2,1)S(1)}, u32[]{:S(2)}, u32[]{:S(2)}) collective-permute-start(bf16[6,1,4,32,128]{4,3,2,1,0:T(8,128)(2,1)} %get-tuple-element.47), channel_id=1, source_target_pairs={{0,4},{4,8},{8,12},{12,0},{1,5},{5,9},{9,13},{13,1},{2,6},{6,10},{... | collective-permute-start | bytes 589832 | tf_op jit(solution)/shard_map/ppermute | solution.py:14
  98.2 113.5 %copy-start.6 = (bf16[8,2,4,1536]{3,2,1,0:T(4,128)(2,1)}, bf16[8,2,4,1536]{3,2,1,0:T(4,128)(2,1)S(1)}, u32[]{:S(2)}) copy-start(bf16[8,2,4,1536]{3,2,1,0:T(4,128)(2,1)S(1)} %collective-permute-done.8) | copy-start | bytes 589828
  98.2 113.5 %collective-permute-start.3 = (bf16[6,1,4,32,128]{4,3,2,1,0:T(8,128)(2,1)}, bf16[6,1,4,32,128]{4,3,2,1,0:T(8,128)(2,1)S(1)}, u32[]{:S(2)}, u32[]{:S(2)}) collective-permute-start(bf16[6,1,4,32,128]{4,3,2,1,0:T(8,128)(2,1)} %get-tuple-element.48), channel_id=1, source_target_pairs={{4,0},{8,4},{12,8},{0,12},{5,1},{9,5},{13,9},{1,13},{6,2},{10,6},{... | collective-permute-start | bytes 589832 | tf_op jit(solution)/shard_map/ppermute | solution.py:15
  102.2 140.3 %collective-permute-start.10 = (bf16[8,8,2,1536]{3,2,1,0:T(2,128)(2,1)}, bf16[8,8,2,1536]{3,2,1,0:T(2,128)(2,1)}, u32[]{:S(2)}, u32[]{:S(2)}) collective-permute-start(bf16[8,8,2,1536]{3,2,1,0:T(2,128)(2,1)} %get-tuple-element.45), channel_id=1, source_target_pairs={{0,1},{1,2},{2,3},{3,0},{4,5},{5,6},{6,7},{7,4},{8,9},{9,10},{10,1... | collective-permute-start | bytes 1179656 | tf_op jit(solution)/shard_map/ppermute | solution.py:14
  103.7 138.8 %collective-permute-start.11 = (bf16[8,8,2,1536]{3,2,1,0:T(2,128)(2,1)}, bf16[8,8,2,1536]{3,2,1,0:T(2,128)(2,1)}, u32[]{:S(2)}, u32[]{:S(2)}) collective-permute-start(bf16[8,8,2,1536]{3,2,1,0:T(2,128)(2,1)} %get-tuple-element.46), channel_id=1, source_target_pairs={{1,0},{2,1},{3,2},{0,3},{5,4},{6,5},{7,6},{4,7},{9,8},{10,9},{11,1... | collective-permute-start | bytes 1179656 | tf_op jit(solution)/shard_map/ppermute | solution.py:15
  212.7 12.0 %collective-permute-start.4 = (bf16[6,6,1,32,128]{4,3,2,1,0:T(8,128)(2,1)}, bf16[6,6,1,32,128]{4,3,2,1,0:T(8,128)(2,1)}, u32[]{:S(2)}, u32[]{:S(2)}) collective-permute-start(bf16[6,6,1,32,128]{4,3,2,1,0:T(8,128)(2,1)} %get-tuple-element.43), channel_id=1, source_target_pairs={{0,1},{1,2},{2,3},{3,0},{4,5},{5,6},{6,7},{7,4},{8,9},{9,10},{10,1... | collective-permute-start | bytes 884744 | tf_op jit(solution)/shard_map/ppermute | solution.py:14
  212.7 13.8 %collective-permute-start.5 = (bf16[6,6,1,32,128]{4,3,2,1,0:T(8,128)(2,1)}, bf16[6,6,1,32,128]{4,3,2,1,0:T(8,128)(2,1)}, u32[]{:S(2)}, u32[]{:S(2)}) collective-permute-start(bf16[6,6,1,32,128]{4,3,2,1,0:T(8,128)(2,1)} %get-tuple-element.44), channel_id=1, source_target_pairs={{1,0},{2,1},{3,2},{0,3},{5,4},{6,5},{7,6},{4,7},{9,8},{10,9},{11,1... | collective-permute-start | bytes 884744 | tf_op jit(solution)/shard_map/ppermute | solution.py:15
  347.0 29.0 %copy-start.2 = (f32[2,2,2,2,2,2,48,32]{6,7,5,2,4,1,3,0:T(8,128)S(1)}, f32[2,2,2,2,2,2,48,32]{6,7,5,2,4,1,3,0:T(8,128)}, u32[]{:S(2)}) copy-start(f32[2,2,2,2,2,2,48,32]{6,7,5,2,4,1,3,0:T(8,128)} %copy.37) | copy-start | bytes 1179652
  376.0 13.2 %copy-start.1 = (bf16[27,128,128]{2,1,0:T(8,128)(2,1)S(1)}, bf16[27,128,128]{2,1,0:T(8,128)(2,1)}, u32[]{:S(2)}) copy-start(bf16[27,128,128]{2,1,0:T(8,128)(2,1)} %param.12) | copy-start | bytes 2654212
  (9 other events, 67.2 us)
where the time goes:
time: 392 us; the launch traced here: 389 us
  local copies, waits for them, and re-layouts  256 us (65%)
  blocking collectives  67.5 us (17%)
  matrix products  24.6 us (6%)
  starting transfers between devices  23.9 us (6%)
  other arithmetic  9.04 us (2%)
  waiting for transfers between devices  7.36 us (2%)
    gather x192, local copies, waits for them, and re-layouts  202 us
    all_gather x1, blocking collectives, coarse_couple(): piece = lax.all_gather(rows, ('gx', 'gy', 'gz'), axis=0, tiled=True)  67.5 us
    reshape x2, local copies, waits for them, and re-layouts, far_couple(): stacked = stacked.reshape(stacked.shape[:4] + (rank_count, -1))  34.2 us
    ppermute x9, starting transfers between devices, extended_2(): after = lax.ppermute(leading, axis, down)  16.8 us
    dot_general x1, matrix products, far_couple(): jnp.einsum('kij,kxyzjr->xyzir', matrices, stacked, preferred_element_type...  11.9 us
  transfers between devices with their start and end apart: 18, of which 3 were waited for; matrix products, arithmetic and copies ran while one was open for 36% of the time, Pallas kernels for 0%

commit v1 on v0

v1 whole, which is shorter than its diff:
```python
import functools

import jax
import jax.numpy as jnp
from jax import lax
from jax.experimental import pallas as pl
from jax.experimental.pallas import tpu as pltpu
from jax.sharding import PartitionSpec as P

MESH = pl.DeviceIdType.MESH
AXES = ("gx", "gy", "gz")
F32 = jnp.float32
BF16 = jnp.bfloat16
NT = (((1,), (1,)), ((), ()))
NN = (((1,), (0,)), ((), ()))


def dot(a, b, dims):
    return lax.dot_general(a, b, dims, preferred_element_type=F32)


def kernel(
    sizes,
    inverse,
    counts,
    far_offsets,
    charges,
    basis,
    transfer,
    near_hbm,
    coupling_hbm,
    coarse_hbm,
    out,
    ext,
    mom,
    one,
    two,
    near_w,
    coupling_raw,
    coarse_raw,
    far_w,
    coarse_w,
    trans_w,
    basis_w,
    near_acc,
    far_acc,
    one_acc,
    local_sem,
    send_sem,
    recv_sem,
    gsend,
    grecv,
):
    bx, by, bz, rhs, pts = charges.shape
    rank = basis.shape[0]
    half = rhs // 2
    lane = pts // 2
    me = [lax.axis_index(a) for a in AXES]
    steps = coupling_raw.shape[1]
    cells = sizes[0] * sizes[1] * sizes[2]

    near_copy = pltpu.make_async_copy(near_hbm, near_w, local_sem.at[0])
    coupling_copy = pltpu.make_async_copy(coupling_hbm, coupling_raw, local_sem.at[1])
    coarse_copy = pltpu.make_async_copy(coarse_hbm, coarse_raw, local_sem.at[2])
    near_copy.start()
    coupling_copy.start()
    coarse_copy.start()

    barrier = pltpu.get_barrier_semaphore()
    peers = 0
    for axis in range(3):
        for d in range(1, sizes[axis]):
            other = lax.rem(me[axis] + d, sizes[axis])
            pl.semaphore_signal(barrier, inc=1, device_id={AXES[axis]: other}, device_id_type=MESH)
            peers += 1

    lanes = lax.broadcasted_iota(jnp.int32, (rhs, pts), 1)

    def mask_box(b, carry):
        x, y, z = b // (by * bz), b // bz % by, b % bz
        value = charges[x, y, z]
        live = (lanes < counts[x, y, z]).astype(F32).astype(BF16)
        ext[1 + x, 1 + y, 1 + z] = value * live
        return carry

    lax.fori_loop(0, bx * by * bz, mask_box, 0)
    pl.semaphore_wait(barrier, peers)

    def halo(ref, stream, width, axis, order):
        own = [(bx, by, bz), (bx, by, bz), (bx // 2, by // 2, bz // 2)][stream]
        done = order[: order.index(axis)]

        def view(start):
            index = []
            for d in range(3):
                if d == axis:
                    index.append(pl.ds(start, width))
                elif d in done:
                    index.append(pl.ds(0, ref.shape[d]))
                else:
                    index.append(pl.ds(width, own[d]))
            return ref.at[tuple(index)]

        n = own[axis]
        moves = [(n, 0, 1)]
        if ref.shape[axis] == n + 2 * width:
            moves.append((width, width + n, sizes[axis] - 1))
        copies = []
        for k, (src, dst, shift) in enumerate(moves):
            slot = (stream * 3 + axis) * 2 + k
            copies.append(
                pltpu.make_async_remote_copy(
                    src_ref=view(src),
                    dst_ref=view(dst),
                    send_sem=send_sem.at[slot],
                    recv_sem=recv_sem.at[slot],
                    device_id={AXES[axis]: lax.rem(me[axis] + shift, sizes[axis])},
                    device_id_type=MESH,
                )
            )
        return copies

    def gather(axis):
        index = [pl.ds(0, sizes[d]) if d < axis else pl.ds(me[d], 1) for d in range(3)]
        view = two.at[tuple(index)]
        copies = []
        base = sum(sizes[d] - 1 for d in range(axis))
        for d in range(1, sizes[axis]):
            copies.append(
                pltpu.make_async_remote_copy(
                    src_ref=view,
                    dst_ref=view,
                    send_sem=gsend.at[base + d - 1],
                    recv_sem=grecv.at[base + d - 1],
                    device_id={AXES[axis]: lax.rem(me[axis] + d, sizes[axis])},
                    device_id_type=MESH,
                )
            )
        return copies

    def start(copies):
        for c in copies:
            c.start()

    def arrive(copies):
        for c in copies:
            c.wait_recv()

    def gather_arrive(axis):
        base = sum(sizes[d] - 1 for d in range(axis))
        for d in range(1, sizes[axis]):
            source = lax.rem(me[axis] + sizes[axis] - d, sizes[axis])
            index = [pl.ds(0, sizes[k]) if k < axis else pl.ds(me[k], 1) for k in range(3)]
            index[axis] = pl.ds(source, 1)
            view = two.at[tuple(index)]
            pltpu.make_async_remote_copy(
                src_ref=view,
                dst_ref=view,
                send_sem=gsend.at[base + d - 1],
                recv_sem=grecv.at[base + d - 1],
                device_id={AXES[axis]: source},
                device_id_type=MESH,
            ).wait_recv()

    order_c, order_m, order_o = (0, 1, 2), (0, 2, 1), (0, 1, 2)
    ch = [halo(ext, 0, 1, a, order_c) for a in order_c]
    mo = [halo(mom, 1, 2, a, order_m) for a in order_m]
    on = [halo(one, 2, 2, a, order_o) for a in order_o]
    tw = [gather(a) for a in range(3)]

    start(ch[0])

    basis_w[...] = jnp.zeros(basis_w.shape, BF16)
    basis_w[0:rank, 0:pts] = basis[...]
    basis_w[lane : lane + rank, pts : 2 * pts] = basis[...]
    trans_w[...] = jnp.zeros(trans_w.shape, BF16)
    for c in range(8):
        trans_w[c, 0:rank, 0:rank] = transfer[c]
        trans_w[c, lane : lane + rank, lane : lane + rank] = transfer[c]

    def moments(x, carry):
        low = ext[1 + x, 1 : 1 + by, 1 : 1 + bz, 0:half].reshape(by * bz * half, pts)
        high = ext[1 + x, 1 : 1 + by, 1 : 1 + bz, half:rhs].reshape(by * bz * half, pts)
        value = dot(jnp.concatenate([low, high], axis=1), basis_w[...], NT).astype(BF16)
        mom[2 + x, 2 : 2 + by, 2 : 2 + bz] = value.reshape(by, bz, half, pts)
        return carry

    lax.fori_loop(0, bx, moments, 0)
    start(mo[0])

    hx, hy, hz = bx // 2, by // 2, bz // 2
    parents = [(a, b, c) for a in range(hx) for b in range(hy) for c in range(hz)]
    kids = [(i, j, l) for i in range(2) for j in range(2) for l in range(2)]
    total = jnp.zeros((len(parents) * half, pts), F32)
    for number, (i, j, l) in enumerate(kids):
        rows = jnp.concatenate(
            [mom[2 + 2 * a + i, 2 + 2 * b + j, 2 + 2 * c + l] for a, b, c in parents], axis=0
        )
        total = total + dot(rows, trans_w[number], NT)
    value = total.astype(BF16)
    for n, (a, b, c) in enumerate(parents):
        one[2 + a, 2 + b, 2 + c] = value[n * half : (n + 1) * half]
    start(on[0])
    total = jnp.zeros((half, pts), F32)
    for number in range(8):
        total = total + dot(value[number * half : (number + 1) * half], trans_w[number], NT)
    two[me[0], me[1], me[2]] = total.astype(BF16)
    start(tw[0])

    far_w[...] = jnp.zeros(far_w.shape, BF16)
    coarse_w[...] = jnp.zeros(coarse_w.shape, BF16)
    coupling_copy.wait()

    def build_far(t, carry):
        for level in range(2):
            for k in range(2):
                value = coupling_raw[level, 2 * t + k]
                for s in range(2):
                    col = k * pts + s * lane
                    far_w[level, t, s * lane : s * lane + rank, col : col + rank] = value
        return carry

    lax.fori_loop(0, steps // 2, build_far, 0)

    arrive(ch[0])
    start(ch[1])
    arrive(mo[0])
    start(mo[1])
    arrive(on[0])
    start(on[1])
    gather_arrive(0)
    start(tw[1])

    coarse_copy.wait()

    def build_coarse(t, carry):
        for k in range(2):
            r = 2 * t + k
            x, y, z = r // (sizes[1] * sizes[2]), r // sizes[2] % sizes[1], r % sizes[2]
            value = coarse_raw[x, y, z]
            for s in range(2):
                col = k * pts + s * lane
                coarse_w[t, s * lane : s * lane + rank, col : col + rank] = value
        return carry

    lax.fori_loop(0, cells // 2, build_coarse, 0)
    near_copy.wait()

    def window(ox, oy, oz):
        v = ext[pl.ds(ox + 1, bx), pl.ds(oy + 1, by), pl.ds(oz + 1, bz)]
        return v.reshape(bx * by * bz * rhs, pts)

    def near_weight(ox, oy, oz):
        return near_w[inverse[(ox + 1) * 9 + (oy + 1) * 3 + oz + 1]]

    near_acc[...] = dot(window(0, 0, 0), near_weight(0, 0, 0), NT)

    def near_pair(first, second):
        rows = jnp.concatenate([window(*first), window(*second)], axis=1)
        mats = jnp.concatenate([near_weight(*first), near_weight(*second)], axis=1)
        near_acc[...] += dot(rows, mats, NT)

    near_pair((-1, 0, 0), (1, 0, 0))

    arrive(ch[1])
    start(ch[2])
    arrive(mo[1])
    start(mo[2])
    arrive(on[1])
    start(on[2])
    gather_arrive(1)
    start(tw[2])

    def near_middle(t, carry):
        near_pair((t - 1, -1, 0), (t - 1, 1, 0))
        return carry

    lax.fori_loop(0, 3, near_middle, 0)

    arrive(ch[2])

    def near_last(t, carry):
        near_pair((t // 3 - 1, t % 3 - 1, -1), (t // 3 - 1, t % 3 - 1, 1))
        return carry

    lax.fori_loop(0, 9, near_last, 0)

    gather_arrive(2)

    def coarse_step(t, total):
        rows = []
        for k in range(2):
            r = 2 * t + k
            x, y, z = r // (sizes[1] * sizes[2]), r // sizes[2] % sizes[1], r % sizes[2]
            rows.append(
                two[
                    lax.rem(me[0] + x, sizes[0]),
                    lax.rem(me[1] + y, sizes[1]),
                    lax.rem(me[2] + z, sizes[2]),
                ]
            )
        return total + dot(jnp.concatenate(rows, axis=1), coarse_w[t], NT)

    local_two = lax.fori_loop(0, cells // 2, coarse_step, jnp.zeros((half, pts), F32))

    arrive(on[2])

    def far_window(ref, level, e, count):
        ox, oy, oz = (far_offsets[level, e, d] + 2 for d in range(3))
        planes = []
        for i in range(count[0]):
            x = lax.rem(ox + i, ref.shape[0])
            v = ref[x, pl.ds(oy, count[1]), pl.ds(oz, count[2])]
            planes.append(v.reshape(count[1] * count[2] * half, pts))
        return jnp.concatenate(planes, axis=0)

    def far_product(ref, level, t, count):
        rows = [far_window(ref, level, 2 * t + k, count) for k in range(2)]
        return dot(jnp.concatenate(rows, axis=1), far_w[level, t], NT)

    one_acc[...] = jnp.zeros(one_acc.shape, F32)

    def far_one(t, carry):
        one_acc[...] += far_product(one, 1, t, (hx, hy, hz))
        return carry

    lax.fori_loop(0, steps // 2, far_one, 0)

    rounded = local_two.astype(BF16)
    for number in range(8):
        rows = slice(number * half, (number + 1) * half)
        one_acc[rows, :] += dot(rounded, trans_w[number], NN)

    rounded = one_acc[...].astype(BF16)
    for number, (i, j, l) in enumerate(kids):
        value = dot(rounded, trans_w[number], NN)
        for n, (a, b, c) in enumerate(parents):
            box = ((2 * a + i) * by + 2 * b + j) * bz + 2 * c + l
            far_acc[box * half : (box + 1) * half, :] = value[n * half : (n + 1) * half]

    arrive(mo[2])

    def far_zero(t, carry):
        far_acc[...] += far_product(mom, 0, t, (bx, by, bz))
        return carry

    lax.fori_loop(0, steps // 2, far_zero, 0)

    def finish(x, carry):
        span = by * bz * half
        rows = far_acc[pl.ds(pl.multiple_of(x * span, span), span), :].astype(BF16)
        value = dot(rows, basis_w[...], NN)
        for b in range(by * bz):
            y, z = b // bz, b % bz
            live = (lanes < counts[x, y, z]).astype(F32)
            far = jnp.concatenate(
                [
                    value[b * half : (b + 1) * half, 0:pts],
                    value[b * half : (b + 1) * half, pts : 2 * pts],
                ],
                axis=0,
            )
            at = pl.multiple_of((x * by * bz + b) * rhs, rhs)
            out[x, y, z] = (near_acc[pl.ds(at, rhs), :] + far) * live
        return carry

    lax.fori_loop(0, bx, finish, 0)

    for group in ch + mo + on + tw:
        for c in group:
            c.wait_send()


def body(
    sizes,
    charges,
    counts,
    near_offsets,
    near_blocks,
    leaf_basis,
    transfer,
    far_offsets,
    coupling,
    coarse_coupling,
):
    bx, by, bz, rhs, pts = charges.shape
    half = rhs // 2
    stencil = near_offsets.shape[0]
    code = (near_offsets[:, 0] + 1) * 9 + (near_offsets[:, 1] + 1) * 3 + near_offsets[:, 2] + 1
    number = jnp.arange(stencil, dtype=jnp.int32)
    inverse = jnp.sum(
        jnp.where(code[None, :] == number[:, None], number[None, :], 0), axis=1, dtype=jnp.int32
    )
    boxes = bx * by * bz
    hx, hy, hz = bx // 2, by // 2, bz // 2
    one_x = hx + 2 if sizes[0] * hx == hx + 2 else hx + 4
    levels, steps = coupling.shape[:2]
    cells = sizes[0] * sizes[1] * sizes[2]
    peers = sum(sizes) - 3
    smem = pl.BlockSpec(memory_space=pltpu.SMEM)
    vmem = pl.BlockSpec(memory_space=pltpu.VMEM)
    hbm = pl.BlockSpec(memory_space=pl.ANY)
    return pl.pallas_call(
        functools.partial(kernel, sizes),
        out_shape=jax.ShapeDtypeStruct(charges.shape, F32),
        in_specs=[smem, smem, smem, vmem, vmem, vmem, hbm, hbm, hbm],
        out_specs=vmem,
        scratch_shapes=[
            pltpu.VMEM((bx + 2, by + 2, bz + 2, rhs, pts), BF16),
            pltpu.VMEM((bx + 4, by + 4, bz + 4, half, pts), BF16),
            pltpu.VMEM((one_x, hy + 4, hz + 4, half, pts), BF16),
            pltpu.VMEM(tuple(sizes) + (half, pts), BF16),
            pltpu.VMEM(near_blocks.shape, BF16),
            pltpu.VMEM(coupling.shape, BF16),
            pltpu.VMEM(coarse_coupling.shape, BF16),
            pltpu.VMEM((levels, steps // 2, pts, 2 * pts), BF16),
            pltpu.VMEM((cells // 2, pts, 2 * pts), BF16),
            pltpu.VMEM((8, pts, pts), BF16),
            pltpu.VMEM((pts, 2 * pts), BF16),
            pltpu.VMEM((boxes * rhs, pts), F32),
            pltpu.VMEM((boxes * half, pts), F32),
            pltpu.VMEM((hx * hy * hz * half, pts), F32),
            pltpu.SemaphoreType.DMA((3,)),
            pltpu.SemaphoreType.DMA((18,)),
            pltpu.SemaphoreType.DMA((18,)),
            pltpu.SemaphoreType.DMA((peers,)),
            pltpu.SemaphoreType.DMA((peers,)),
        ],
        compiler_params=pltpu.CompilerParams(
            collective_id=0, has_side_effects=True, vmem_limit_bytes=56 * 1024 * 1024
        ),
    )(
        inverse,
        counts,
        far_offsets,
        charges,
        leaf_basis,
        transfer,
        near_blocks,
        coupling,
        coarse_coupling,
    )


def solution(mesh):
    sizes = tuple(mesh.shape[a] for a in AXES)
    in_specs = (
        P("gx", "gy", "gz", None, None),
        P("gx", "gy", "gz"),
        P(),
        P(),
        P(),
        P(),
        P(),
        P(),
        P(),
    )
    out_specs = P("gx", "gy", "gz", None, None)
    return jax.shard_map(
        functools.partial(body, sizes),
        mesh=mesh,
        in_specs=in_specs,
        out_specs=out_specs,
        check_vma=False,
    )
```

time: 392 us -> 73.2 us (0.19)
  local copies, waits for them, and re-layouts: 256 us -> 3 us
  Pallas kernels: 0 us -> 68.4 us
  blocking collectives: 67.5 us -> 0 us
  matrix products: 24.6 us -> 0 us
  starting transfers between devices: 23.9 us -> 0 us
  other arithmetic: 9.04 us -> 1.51 us
  waiting for transfers between devices: 7.36 us -> 0 us
    gather x194 -> x0, local copies, waits for them, and re-layouts: 210 us -> none
    pallas_call x0 -> x1, Pallas kernels: none -> 68.4 us  [body(): pl.pallas_call(functools.partial(kernel, sizes), out_shape=jax.ShapeDtype...]
    all_gather x1 -> x0, blocking collectives: 67.5 us -> none  [coarse_couple(): piece = lax.all_gather(rows, ('gx', 'gy', 'gz'), axis=0, tiled=True)]
    reshape x6 -> x0, local copies, waits for them, and re-layouts: 36.2 us -> none  [the longest x2 34.2 us: far_couple(): stacked = stacked.reshape(stacked.shape[:4] + (rank_count, -1))]
    dot_general x8 -> x0, matrix products: 24.6 us -> none  [the longest x1 11.9 us: far_couple(): jnp.einsum('kij,kxyzjr->xyzir', matrices, stacked, preferred_element_type...]
    ppermute x18 -> x0, starting transfers between devices: 23.9 us -> none  [the longest x9 16.8 us: extended_2(): after = lax.ppermute(leading, axis, down)]
    ppermute x18 -> x0, waiting for transfers between devices: 7.36 us -> none  [the longest x9 5.52 us: extended_2(): before = lax.ppermute(last, axis, up)]
    concatenate x7 -> x0, other arithmetic: 5.48 us -> none  [the longest x5 5.46 us: extended_2(): value = jnp.concatenate([before, value, after], axis=dim)]
  transfers between devices with their start and end apart: 18 -> 0, of which waited for: 3 -> 0; matrix products, arithmetic and copies ran while one was open for 36% -> 0% of each run, Pallas kernels for 0% -> 0%
where the time goes in v1:
time: 73.2 us; the launch traced here: 73 us
  Pallas kernels  68.4 us (93%)
  local copies, waits for them, and re-layouts  3 us (4%)
  other arithmetic  1.51 us (2%)
    pallas_call x1, Pallas kernels, body(): pl.pallas_call(functools.partial(kernel, sizes), out_shape=jax.ShapeDtype...  68.4 us
    unnamed x4, local copies, waits for them, and re-layouts  3 us

profile of v1, /device:TPU:0, one launch (start us, length us, event | category | flops | bytes accessed | tf_op | source)
XLA Modules:
  0.0 73.0 jit_solution(3422595094686815109)
XLA Ops:
  0.0 0.0 copy-start
  0.0 0.8 %add_bitcast_fusion = s32[27]{0:T(128)S(1)} fusion(s32[27,3]{0,1:T(4,128)} %param.11), kind=kLoop, calls=%fused_computation.2 | loop fusion | flops 189 | bytes 432 | tf_op jit(solution)/shard_map/add | solution.py:389
  0.8 0.7 select_reduce_fusion.inverse
  1.5 0.0 copy-done
  1.5 0.7 copy.11.far_offsets
  2.2 68.4 %shard_map.91 = f32[4,4,4,32,128]{4,3,2,1,0:T(8,128)} custom-call(s32[27]{0:T(128)} %select_reduce_fusion.inverse, s32[4,4,4]{2,1,0:T(4,128)} %counts.1, s32[2,32,3]{2,1,0:T(8,128)} %copy.11.far_offsets, bf16[4,4,4,32,128]{4,3,2,1,0:T(8,128)(2,1)} %charges.1, bf16[48,128]{1,0:T(8,128)(2,1)} %basis.1, bf16[8,48,48]{2,1,0:T(8,128)(2,1)} %transfer.1, ...), custom_call_target="tpu_custom_call" | custom-call | tf_op jit(solution)/shard_map/pallas_call | solution.py:403
  70.7 2.3 %copy.13 = f32[4,4,4,32,128]{4,3,2,1,0:T(8,128)} copy(f32[4,4,4,32,128]{4,3,2,1,0:T(8,128)} %shard_map.91) | data formatting | bytes 2097152
Async XLA Ops:
  0.0 1.5 %copy-start = (s32[2,32,3]{1,0,2:T(2,128)S(1)}, s32[2,32,3]{1,0,2:T(2,128)}, u32[]{:S(2)}) copy-start(s32[2,32,3]{1,0,2:T(2,128)} %param.15) | copy-start | bytes 2308

commit v2 on v1

--- a/solution.py
+++ b/solution.py
@@ -21,7 +21,7 @@
 
 def kernel(
     sizes,
-    inverse,
+    near_offsets,
     counts,
     far_offsets,
     charges,
@@ -45,6 +45,8 @@
     near_acc,
     far_acc,
     one_acc,
+    code,
+    inverse,
     local_sem,
     send_sem,
     recv_sem,
@@ -86,39 +88,49 @@
     lax.fori_loop(0, bx * by * bz, mask_box, 0)
     pl.semaphore_wait(barrier, peers)
 
-    def halo(ref, stream, width, axis, order):
+    def halo(ref, stream, width, order):
         own = [(bx, by, bz), (bx, by, bz), (bx // 2, by // 2, bz // 2)][stream]
-        done = order[: order.index(axis)]
-
-        def view(start):
-            index = []
-            for d in range(3):
-                if d == axis:
-                    index.append(pl.ds(start, width))
-                elif d in done:
-                    index.append(pl.ds(0, ref.shape[d]))
-                else:
-                    index.append(pl.ds(width, own[d]))
-            return ref.at[tuple(index)]
-
-        n = own[axis]
-        moves = [(n, 0, 1)]
-        if ref.shape[axis] == n + 2 * width:
-            moves.append((width, width + n, sizes[axis] - 1))
-        copies = []
-        for k, (src, dst, shift) in enumerate(moves):
-            slot = (stream * 3 + axis) * 2 + k
-            copies.append(
-                pltpu.make_async_remote_copy(
-                    src_ref=view(src),
-                    dst_ref=view(dst),
-                    send_sem=send_sem.at[slot],
-                    recv_sem=recv_sem.at[slot],
-                    device_id={AXES[axis]: lax.rem(me[axis] + shift, sizes[axis])},
-                    device_id_type=MESH,
+        high = [ref.shape[d] == own[d] + 2 * width for d in range(3)]
+        part = {
+            "o": lambda d: pl.ds(width, own[d]),
+            "l": lambda d: pl.ds(0, width),
+            "h": lambda d: pl.ds(width + own[d], width),
+            "f": lambda d: pl.ds(0, ref.shape[d]),
+        }
+        first, second, third = order
+        plans = [("A", first, {}), ("B", second, {first: "o"})]
+        plans += [("Bs", second, {first: side}) for side in "lh"]
+        plans += [("C", third, {first: "o", second: "o"})]
+        plans += [("Cs", third, {first: side, second: "o"}) for side in "lh"]
+        plans += [("Cf", third, {first: "f", second: side}) for side in "lh"]
+        groups = {"A": [], "B": [], "Bs": [], "C": [], "Cs": [], "Cf": []}
+        slot = stream * 18
+        for name, axis, fixed in plans:
+            if any(side == "h" and not high[d] for d, side in fixed.items()):
+                continue
+
+            def view(start):
+                index = [part[fixed.get(d, "o")](d) for d in range(3)]
+                index[axis] = pl.ds(start, width)
+                return ref.at[tuple(index)]
+
+            n = own[axis]
+            moves = [(n, 0, 1)]
+            if high[axis]:
+                moves.append((width, width + n, sizes[axis] - 1))
+            for src, dst, shift in moves:
+                groups[name].append(
+                    pltpu.make_async_remote_copy(
+                        src_ref=view(src),
+                        dst_ref=view(dst),
+                        send_sem=send_sem.at[slot],
+                        recv_sem=recv_sem.at[slot],
+                        device_id={AXES[axis]: lax.rem(me[axis] + shift, sizes[axis])},
+                        device_id_type=MESH,
+                    )
                 )
-            )
-        return copies
+                slot += 1
+        return groups
 
     def gather(axis):
         index = [pl.ds(0, sizes[d]) if d < axis else pl.ds(me[d], 1) for d in range(3)]
@@ -162,13 +174,30 @@
                 device_id_type=MESH,
             ).wait_recv()
 
-    order_c, order_m, order_o = (0, 1, 2), (0, 2, 1), (0, 1, 2)
-    ch = [halo(ext, 0, 1, a, order_c) for a in order_c]
-    mo = [halo(mom, 1, 2, a, order_m) for a in order_m]
-    on = [halo(one, 2, 2, a, order_o) for a in order_o]
+    ch = halo(ext, 0, 1, (0, 1, 2))
+    mo = halo(mom, 1, 2, (0, 2, 1))
+    on = halo(one, 2, 2, (0, 1, 2))
     tw = [gather(a) for a in range(3)]
 
-    start(ch[0])
+    def begin(groups):
+        for name in ("A", "B", "C"):
+            start(groups[name])
+
+    def middle(groups):
+        arrive(groups["A"])
+        start(groups["Bs"])
+        start(groups["Cs"])
+
+    def corner(groups):
+        arrive(groups["B"])
+        arrive(groups["Bs"])
+        start(groups["Cf"])
+
+    def ending(groups):
+        for name in ("C", "Cs", "Cf"):
+            arrive(groups[name])
+
+    begin(ch)
 
     basis_w[...] = jnp.zeros(basis_w.shape, BF16)
     basis_w[0:rank, 0:pts] = basis[...]
@@ -186,7 +215,7 @@
         return carry
 
     lax.fori_loop(0, bx, moments, 0)
-    start(mo[0])
+    begin(mo)
 
     hx, hy, hz = bx // 2, by // 2, bz // 2
     parents = [(a, b, c) for a in range(hx) for b in range(hy) for c in range(hz)]
@@ -200,34 +229,44 @@
     value = total.astype(BF16)
     for n, (a, b, c) in enumerate(parents):
         one[2 + a, 2 + b, 2 + c] = value[n * half : (n + 1) * half]
-    start(on[0])
+    begin(on)
     total = jnp.zeros((half, pts), F32)
     for number in range(8):
         total = total + dot(value[number * half : (number + 1) * half], trans_w[number], NT)
     two[me[0], me[1], me[2]] = total.astype(BF16)
     start(tw[0])
 
+    stencil = near_offsets.shape[1]
+    for number in range(stencil):
+        x, y, z = (near_offsets[d, number] + 1 for d in range(3))
+        code[number] = x * 9 + y * 3 + z
+
+    def invert(c, carry):
+        found = jnp.int32(0)
+        for number in range(stencil):
+            found = found + jnp.where(code[number] == c, number, 0)
+        inverse[c] = jnp.minimum(found, stencil - 1)
+        return carry
+
+    lax.fori_loop(0, stencil, invert, 0)
     far_w[...] = jnp.zeros(far_w.shape, BF16)
     coarse_w[...] = jnp.zeros(coarse_w.shape, BF16)
     coupling_copy.wait()
 
     def build_far(t, carry):
         for level in range(2):
-            for k in range(2):
-                value = coupling_raw[level, 2 * t + k]
+            for k in range(4):
+                value = coupling_raw[level, 4 * t + k]
                 for s in range(2):
                     col = k * pts + s * lane
                     far_w[level, t, s * lane : s * lane + rank, col : col + rank] = value
         return carry
 
-    lax.fori_loop(0, steps // 2, build_far, 0)
-
-    arrive(ch[0])
-    start(ch[1])
-    arrive(mo[0])
-    start(mo[1])
-    arrive(on[0])
-    start(on[1])
+    lax.fori_loop(0, steps // 4, build_far, 0)
+
+    middle(ch)
+    middle(mo)
+    middle(on)
     gather_arrive(0)
     start(tw[1])
 
@@ -262,12 +301,9 @@
 
     near_pair((-1, 0, 0), (1, 0, 0))
 
-    arrive(ch[1])
-    start(ch[2])
-    arrive(mo[1])
-    start(mo[2])
-    arrive(on[1])
-    start(on[2])
+    corner(ch)
+    corner(mo)
+    corner(on)
     gather_arrive(1)
     start(tw[2])
 
@@ -277,7 +313,7 @@
 
     lax.fori_loop(0, 3, near_middle, 0)
 
-    arrive(ch[2])
+    ending(ch)
 
     def near_last(t, carry):
         near_pair((t // 3 - 1, t % 3 - 1, -1), (t // 3 - 1, t % 3 - 1, 1))
@@ -303,10 +339,10 @@
 
     local_two = lax.fori_loop(0, cells // 2, coarse_step, jnp.zeros((half, pts), F32))
 
-    arrive(on[2])
+    ending(on)
 
     def far_window(ref, level, e, count):
-        ox, oy, oz = (far_offsets[level, e, d] + 2 for d in range(3))
+        ox, oy, oz = (far_offsets[d, level, e] + 2 for d in range(3))
         planes = []
         for i in range(count[0]):
             x = lax.rem(ox + i, ref.shape[0])
@@ -315,7 +351,7 @@
         return jnp.concatenate(planes, axis=0)
 
     def far_product(ref, level, t, count):
-        rows = [far_window(ref, level, 2 * t + k, count) for k in range(2)]
+        rows = [far_window(ref, level, 4 * t + k, count) for k in range(4)]
         return dot(jnp.concatenate(rows, axis=1), far_w[level, t], NT)
 
     one_acc[...] = jnp.zeros(one_acc.shape, F32)
@@ -324,7 +360,7 @@
         one_acc[...] += far_product(one, 1, t, (hx, hy, hz))
         return carry
 
-    lax.fori_loop(0, steps // 2, far_one, 0)
+    lax.fori_loop(0, steps // 4, far_one, 0)
 
     rounded = local_two.astype(BF16)
     for number in range(8):
@@ -338,13 +374,13 @@
             box = ((2 * a + i) * by + 2 * b + j) * bz + 2 * c + l
             far_acc[box * half : (box + 1) * half, :] = value[n * half : (n + 1) * half]
 
-    arrive(mo[2])
+    ending(mo)
 
     def far_zero(t, carry):
         far_acc[...] += far_product(mom, 0, t, (bx, by, bz))
         return carry
 
-    lax.fori_loop(0, steps // 2, far_zero, 0)
+    lax.fori_loop(0, steps // 4, far_zero, 0)
 
     def finish(x, carry):
         span = by * bz * half
@@ -366,7 +402,8 @@
 
     lax.fori_loop(0, bx, finish, 0)
 
-    for group in ch + mo + on + tw:
+    groups = list(ch.values()) + list(mo.values()) + list(on.values()) + tw
+    for group in groups:
         for c in group:
             c.wait_send()
 
@@ -386,11 +423,6 @@
     bx, by, bz, rhs, pts = charges.shape
     half = rhs // 2
     stencil = near_offsets.shape[0]
-    code = (near_offsets[:, 0] + 1) * 9 + (near_offsets[:, 1] + 1) * 3 + near_offsets[:, 2] + 1
-    number = jnp.arange(stencil, dtype=jnp.int32)
-    inverse = jnp.sum(
-        jnp.where(code[None, :] == number[:, None], number[None, :], 0), axis=1, dtype=jnp.int32
-    )
     boxes = bx * by * bz
     hx, hy, hz = bx // 2, by // 2, bz // 2
     one_x = hx + 2 if sizes[0] * hx == hx + 2 else hx + 4
@@ -413,16 +445,18 @@
             pltpu.VMEM(near_blocks.shape, BF16),
             pltpu.VMEM(coupling.shape, BF16),
             pltpu.VMEM(coarse_coupling.shape, BF16),
-            pltpu.VMEM((levels, steps // 2, pts, 2 * pts), BF16),
+            pltpu.VMEM((levels, steps // 4, pts, 4 * pts), BF16),
             pltpu.VMEM((cells // 2, pts, 2 * pts), BF16),
             pltpu.VMEM((8, pts, pts), BF16),
             pltpu.VMEM((pts, 2 * pts), BF16),
             pltpu.VMEM((boxes * rhs, pts), F32),
             pltpu.VMEM((boxes * half, pts), F32),
             pltpu.VMEM((hx * hy * hz * half, pts), F32),
+            pltpu.SMEM((stencil,), jnp.int32),
+            pltpu.SMEM((stencil,), jnp.int32),
             pltpu.SemaphoreType.DMA((3,)),
-            pltpu.SemaphoreType.DMA((18,)),
-            pltpu.SemaphoreType.DMA((18,)),
+            pltpu.SemaphoreType.DMA((54,)),
+            pltpu.SemaphoreType.DMA((54,)),
             pltpu.SemaphoreType.DMA((peers,)),
             pltpu.SemaphoreType.DMA((peers,)),
         ],
@@ -430,9 +464,9 @@
             collective_id=0, has_side_effects=True, vmem_limit_bytes=56 * 1024 * 1024
         ),
     )(
-        inverse,
+        near_offsets.T,
         counts,
-        far_offsets,
+        far_offsets.transpose(2, 0, 1),
         charges,
         leaf_basis,
         transfer,

time: 73.2 us -> 55.5 us (0.76)
  Pallas kernels: 68.4 us -> 53.1 us
  other arithmetic: 1.51 us -> 0 us
    pallas_call x1, Pallas kernels: 68.4 us -> 53.1 us  [body(): pl.pallas_call(functools.partial(kernel, sizes), out_shape=jax.ShapeDtype...]
    add x1 -> x0, other arithmetic: 0.8 us -> none  [body(): (near_offsets[:, 0] + 1) * 9 + (near_offsets[:, 1] + 1) * 3]
    unnamed x4 -> x1, local copies, waits for them, and re-layouts: 3 us -> 2.29 us
where the time goes in v2:
time: 55.5 us; the launch traced here: 55.4 us
  Pallas kernels  53.1 us (96%)
  local copies, waits for them, and re-layouts  2.29 us (4%)
    pallas_call x1, Pallas kernels, body(): pl.pallas_call(functools.partial(kernel, sizes), out_shape=jax.ShapeDtype...  53.1 us
    unnamed x1, local copies, waits for them, and re-layouts  2.29 us

profile of v2, /device:TPU:0, one launch (start us, length us, event | category | flops | bytes accessed | tf_op | source)
XLA Modules:
  0.0 55.4 jit_solution(17538313155626519459)
XLA Ops:
  0.0 53.1 %shard_map.91 = f32[4,4,4,32,128]{4,3,2,1,0:T(8,128)} custom-call(s32[3,27]{1,0:T(4,128)} %bitcast.3, s32[4,4,4]{2,1,0:T(4,128)} %counts.1, s32[3,2,32]{2,1,0:T(2,128)} %bitcast.2, bf16[4,4,4,32,128]{4,3,2,1,0:T(8,128)(2,1)} %charges.1, bf16[48,128]{1,0:T(8,128)(2,1)} %basis.1, bf16[8,48,48]{2,1,0:T(8,128)(2,1)} %transfer.1, bf16[27,128,128]{2,1,0:T(8,128)(2,1)} %near_hbm.1, ...), custom_call_target="tpu_custom_call" | custom-call | tf_op jit(solution)/shard_map/pallas_call | solution.py:435
  53.1 2.3 %copy.11 = f32[4,4,4,32,128]{4,3,2,1,0:T(8,128)} copy(f32[4,4,4,32,128]{4,3,2,1,0:T(8,128)} %shard_map.91) | data formatting | bytes 2097152

commit v3 on v2

--- a/solution.py
+++ b/solution.py
@@ -86,7 +86,6 @@
         return carry
 
     lax.fori_loop(0, bx * by * bz, mask_box, 0)
-    pl.semaphore_wait(barrier, peers)
 
     def halo(ref, stream, width, order):
         own = [(bx, by, bz), (bx, by, bz), (bx // 2, by // 2, bz // 2)][stream]
@@ -184,20 +183,20 @@
             start(groups[name])
 
     def middle(groups):
-        arrive(groups["A"])
-        start(groups["Bs"])
-        start(groups["Cs"])
+        for k, copy in enumerate(groups["A"]):
+            copy.wait_recv()
+            start(groups["Bs"][2 * k : 2 * k + 2])
+            start(groups["Cs"][2 * k : 2 * k + 2])
 
     def corner(groups):
-        arrive(groups["B"])
-        arrive(groups["Bs"])
-        start(groups["Cf"])
+        for k in range(2):
+            arrive(groups["B"][k::2])
+            arrive(groups["Bs"][k::2])
+            start(groups["Cf"][2 * k : 2 * k + 2])
 
     def ending(groups):
         for name in ("C", "Cs", "Cf"):
             arrive(groups[name])
-
-    begin(ch)
 
     basis_w[...] = jnp.zeros(basis_w.shape, BF16)
     basis_w[0:rank, 0:pts] = basis[...]
@@ -215,6 +214,7 @@
         return carry
 
     lax.fori_loop(0, bx, moments, 0)
+    pl.semaphore_wait(barrier, peers)
     begin(mo)
 
     hx, hy, hz = bx // 2, by // 2, bz // 2
@@ -235,6 +235,7 @@
         total = total + dot(value[number * half : (number + 1) * half], trans_w[number], NT)
     two[me[0], me[1], me[2]] = total.astype(BF16)
     start(tw[0])
+    begin(ch)
 
     stencil = near_offsets.shape[1]
     for number in range(stencil):
@@ -264,7 +265,6 @@
 
     lax.fori_loop(0, steps // 4, build_far, 0)
 
-    middle(ch)
     middle(mo)
     middle(on)
     gather_arrive(0)
@@ -299,27 +299,19 @@
         mats = jnp.concatenate([near_weight(*first), near_weight(*second)], axis=1)
         near_acc[...] += dot(rows, mats, NT)
 
-    near_pair((-1, 0, 0), (1, 0, 0))
-
-    corner(ch)
-    corner(mo)
-    corner(on)
     gather_arrive(1)
     start(tw[2])
+    corner(on)
+    corner(mo)
+    middle(ch)
+    near_pair((-1, 0, 0), (1, 0, 0))
+    corner(ch)
 
     def near_middle(t, carry):
         near_pair((t - 1, -1, 0), (t - 1, 1, 0))
         return carry
 
     lax.fori_loop(0, 3, near_middle, 0)
-
-    ending(ch)
-
-    def near_last(t, carry):
-        near_pair((t // 3 - 1, t % 3 - 1, -1), (t // 3 - 1, t % 3 - 1, 1))
-        return carry
-
-    lax.fori_loop(0, 9, near_last, 0)
 
     gather_arrive(2)
 
@@ -374,6 +366,15 @@
             box = ((2 * a + i) * by + 2 * b + j) * bz + 2 * c + l
             far_acc[box * half : (box + 1) * half, :] = value[n * half : (n + 1) * half]
 
+    arrive(ch["C"])
+    arrive(ch["Cs"])
+
+    def near_side(t, carry):
+        near_pair((t - 1, 0, -1), (t - 1, 0, 1))
+        return carry
+
+    lax.fori_loop(0, 3, near_side, 0)
+
     ending(mo)
 
     def far_zero(t, carry):
@@ -381,6 +382,15 @@
         return carry
 
     lax.fori_loop(0, steps // 4, far_zero, 0)
+
+    arrive(ch["Cf"])
+
+    def near_corner(t, carry):
+        x, y = t // 2 - 1, t % 2 * 2 - 1
+        near_pair((x, y, -1), (x, y, 1))
+        return carry
+
+    lax.fori_loop(0, 6, near_corner, 0)
 
     def finish(x, carry):
         span = by * bz * half

time: 55.5 us -> 52.6 us (0.948)
  Pallas kernels: 53.1 us -> 50 us
    pallas_call x1, Pallas kernels: 53.1 us -> 50 us  [body(): pl.pallas_call(functools.partial(kernel, sizes), out_shape=jax.ShapeDtype...]
where the time goes in v3:
time: 52.6 us; the launch traced here: 52.3 us
  Pallas kernels  50 us (95%)
  local copies, waits for them, and re-layouts  2.29 us (4%)
    pallas_call x1, Pallas kernels, body(): pl.pallas_call(functools.partial(kernel, sizes), out_shape=jax.ShapeDtype...  50 us
    unnamed x1, local copies, waits for them, and re-layouts  2.29 us

profile of v3, /device:TPU:0, one launch (start us, length us, event | category | flops | bytes accessed | tf_op | source)
XLA Modules:
  0.0 52.3 jit_solution(1986450943998083055)
XLA Ops:
  0.0 50.0 %shard_map.91 = f32[4,4,4,32,128]{4,3,2,1,0:T(8,128)} custom-call(s32[3,27]{1,0:T(4,128)} %bitcast.3, s32[4,4,4]{2,1,0:T(4,128)} %counts.1, s32[3,2,32]{2,1,0:T(2,128)} %bitcast.2, bf16[4,4,4,32,128]{4,3,2,1,0:T(8,128)(2,1)} %charges.1, bf16[48,128]{1,0:T(8,128)(2,1)} %basis.1, bf16[8,48,48]{2,1,0:T(8,128)(2,1)} %transfer.1, bf16[27,128,128]{2,1,0:T(8,128)(2,1)} %near_hbm.1, ...), custom_call_target="tpu_custom_call" | custom-call | tf_op jit(solution)/shard_map/pallas_call | solution.py:445
  50.0 2.3 %copy.11 = f32[4,4,4,32,128]{4,3,2,1,0:T(8,128)} copy(f32[4,4,4,32,128]{4,3,2,1,0:T(8,128)} %shard_map.91) | data formatting | bytes 2097152
